TPU v7x, 512 devices: a whole 4x8x8 slice. The times are simulated.
512 devices in a mesh: fsdp: 128 (over y, z, core), dp: 4 (over x).
Axes of the slice: x: 4, y: 8, z: 8, core: 2. Of those that a mesh axis runs over, the one named last changes fastest.
Arguments:
- tokens: bfloat16 [512, 4096], P('dp', 'fsdp'), may hold values from -6 to 6
- out_grad: bfloat16 [512, 5120], P('dp', 'fsdp'), may hold values from -0.26367188 to 0.26367188
- master: float32 [4096, 5120], P('fsdp'), may hold values from -0.09375 to 0.09375
- moment_one: float32 [4096, 5120], P('fsdp'), may hold values from -3 to 3
- moment_two: float32 [4096, 5120], P('fsdp'), may hold values from 0.1 to 4
- flags: int32 [512, 16], P(('fsdp', 'dp')), may hold values 0 or 1
- steps: int32 [16], replicated, may hold values from 1 to 8
- rate: float32 [1], replicated, may hold values from 0.001 to 0.01
Outputs:
- master_next: float32 [4096, 5120], P('fsdp')
- moment_one_next: float32 [4096, 5120], P('fsdp')
- moment_two_next: float32 [4096, 5120], P('fsdp')
- weight_half: bfloat16 [4096, 5120], P('fsdp')
- steps_next: int32 [16], replicated
- outputs: bfloat16 [512, 5120], P('dp', 'fsdp')
All inputs are finite; a program needn't handle non-finite values. No bound on the sum of `flags` on one device may be relied on, other than what follows from the above.
Results may differ from a plain program's by a relative error of at most 0.0049.
Values may be sent and summed in bfloat16 or wider, within the bound.
No kernel may reach another device: no remote copies, remote signals or barrier semaphores. Data moves between devices by JAX's collectives and lax.ppermute only.
A program may use at most 64 MiB of HBM per device.

v0:
```python
import jax
import jax.numpy as jnp
from jax import lax
from jax.sharding import Mesh
from jax.sharding import PartitionSpec as P

BUCKETS = 16
FSDP = ("fsdp_0", "fsdp_1", "fsdp_2")
FSDP_DP = ("fsdp_0", "fsdp_1", "fsdp_2", "dp")
first_decay = 0.9
second_decay = 0.95
epsilon = 1e-08


def joined_along(blocks, dim):
    blocks = jnp.moveaxis(blocks, 0, dim)
    shape = blocks.shape
    return blocks.reshape(*shape[:dim], shape[dim] * shape[dim + 1], *shape[dim + 2 :])


def all_blocks(x, axes, order):
    blocks = x[None]
    for k in order:
        blocks = lax.all_gather(blocks, axes[k], axis=0, tiled=True)
    current = [lax.axis_size(axes[k]) for k in reversed(order)]
    blocks = blocks.reshape(*current, *x.shape)
    turned = sorted(range(len(order)), key=lambda place: order[len(order) - 1 - place])
    return blocks.transpose(*turned, *range(len(order), blocks.ndim)).reshape(-1, *x.shape)


def gather_axes(x, axes, order, dim):
    return joined_along(all_blocks(x, axes, order), dim)


def over_axes(x, axes):
    for axis in axes:
        x = lax.psum(x, axis)
    return x


def from_everyone(x, axis):
    size = lax.axis_size(axis)
    return lax.all_to_all(jnp.broadcast_to(x[None], (size, *x.shape)), axis, 0, 0, tiled=True)


def of_everyone(x, axis):
    everything = from_everyone(x, axis)
    return jnp.sum(everything, axis=0)


def local(tokens, out_grad, master, moment_one, moment_two, flags, steps, rate):
    width_out = master.shape[1]
    bucket_width = width_out // BUCKETS
    contract_rows = (((0,), (0,)), ((), ()))
    partial_value = lax.dot_general(
        tokens,
        gather_axes(out_grad, (("fsdp_0", "fsdp_1"), "fsdp_2"), (0, 1), 1),
        contract_rows,
        preferred_element_type=jnp.float32,
    )
    counts = over_axes(flags[0], FSDP_DP)
    gradient = of_everyone(partial_value, "dp")
    commit_bucket = counts == 0
    commit = jnp.repeat(commit_bucket, bucket_width)[None, :]
    times = jnp.repeat(steps + 1, bucket_width).astype(jnp.float32)[None, :]
    first = first_decay * moment_one + (1.0 - first_decay) * gradient
    second = second_decay * moment_two + (1.0 - second_decay) * gradient * gradient
    fix_one = 1.0 - jnp.power(jnp.float32(first_decay), times)
    fix_two = 1.0 - jnp.power(jnp.float32(second_decay), times)
    candidate = master - rate[0] * (first / fix_one) / (jnp.sqrt(second / fix_two) + epsilon)
    master_next = jnp.where(commit, candidate, master)
    moment_one_next = jnp.where(commit, first, moment_one)
    moment_two_next = jnp.where(commit, second, moment_two)
    weight_half = master_next.astype(jnp.bfloat16)
    steps_next = steps + commit_bucket.astype(jnp.int32)
    weight_cols = lax.all_to_all(weight_half, FSDP, split_axis=1, concat_axis=0, tiled=True)
    result = jnp.dot(
        lax.all_gather(tokens, FSDP, axis=1, tiled=True),
        weight_cols,
        preferred_element_type=jnp.float32,
    )
    return (
        master_next,
        moment_one_next,
        moment_two_next,
        weight_half,
        steps_next,
        result.astype(jnp.bfloat16),
    )


def solution(mesh):
    split = Mesh(
        mesh.devices.reshape(8, 8, 2, mesh.shape["dp"]), ("fsdp_0", "fsdp_1", "fsdp_2", "dp")
    )
    in_specs = (
        P("dp", FSDP),
        P("dp", FSDP),
        P(FSDP, None),
        P(FSDP, None),
        P(FSDP, None),
        P(FSDP_DP, None),
        P(),
        P(),
    )
    out_specs = (P(FSDP, None), P(FSDP, None), P(FSDP, None), P(FSDP, None), P(), P("dp", FSDP))
    return jax.shard_map(local, mesh=split, in_specs=in_specs, out_specs=out_specs, check_vma=False)
```

profile of v0, /device:TPU:1, one launch (start us, length us, event | category | flops | bytes accessed | tf_op | source)
XLA Modules:
  0.0 188.4 jit_solution(5304647750274123168)
XLA Ops:
  8.0 0.0 all-gather.4.cloned.1.call-start
  8.0 47.0 %all-gather = bf16[8192,40]{0,1:T(8,128)(2,1)S(1)} all-gather(bf16[128,40]{0,1:T(8,128)(2,1)} %param.9), channel_id=2, replica_groups=mesh['fsdp_0'=8,'fsdp_1'=8,'fsdp_2'=2,'dp'=4] {'fsdp_0','fsdp_1'}, dimensions={0}, use_global_device_ids=true | all-gather | bytes 665600 | tf_op jit(solution)/shard_map/all_gather | solution.py:24
  55.1 1.0 copy.30
  56.1 0.0 all-gather.4.cloned.1.call-update
  56.1 26.5 %all-gather.4.cloned.1.call-done = bf16[128,128,40]{1,0,2:T(8,128)(2,1)} async-done(((bf16[64,128,40]{1,0,2:T(8,128)(2,1)}), bf16[128,128,40]{1,0,2:T(8,128)(2,1)}) %all-gather.4.cloned.1.call-update) | async-done | bytes 1310736 | tf_op jit(solution)/shard_map/all_gather | solution.py:24
  82.6 2.2 %copy.25 = bf16[64,2,128,40]{2,3,1,0:T(8,128)(2,1)S(1)} copy(bf16[64,2,128,40]{2,0,1,3:T(8,128)(2,1)} %bitcast.33) | data formatting | bytes 2621440 | tf_op jit(solution)/shard_map/transpose | solution.py:28
  84.8 0.5 fusion.5
  85.3 1.8 broadcast_in_dim.38
  87.1 3.8 %all-to-all-start = ((f32[4,32,5120]{2,1,0:T(8,128)}), f32[4,32,5120]{2,1,0:T(8,128)S(1)}, u32[]{:S(2)}, u32[]{:S(2)}) async-start(f32[4,32,5120]{2,1,0:T(8,128)} %broadcast_in_dim.38), calls=%async_computation | async-start | bytes 5242880 | tf_op jit(solution)/shard_map/all_to_all | solution.py:43
  90.9 0.0 all-gather.6.cloned.1.call-start
  91.0 0.5 all-gather.6.cloned.1.call-update
  91.5 0.1 broadcast_in_dim.40
  91.6 0.1 sub.30
  91.7 0.1 broadcast_in_dim.39
  91.7 0.1 sub.28
  92.5 10.5 %psum.28 = s32[16]{0:T(128)S(1)} all-reduce(s32[16]{0:T(128)S(1)} %bitcast.34), channel_id=1, replica_groups=mesh['fsdp_0'=8,'fsdp_1'=8,'fsdp_2'=2,'dp'=4] {'fsdp_0'}, use_global_device_ids=true, to_apply=%region_0.0 | all-reduce | flops 16 | bytes 128 | tf_op jit(solution)/shard_map/psum | solution.py:37
  103.0 12.2 %psum.29 = s32[16]{0:T(128)S(1)} all-reduce(s32[16]{0:T(128)S(1)} %psum.28), channel_id=1, replica_groups=mesh['fsdp_0'=8,'fsdp_1'=8,'fsdp_2'=2,'dp'=4] {'fsdp_1'}, use_global_device_ids=true, to_apply=%region_1.0 | all-reduce | flops 16 | bytes 128 | tf_op jit(solution)/shard_map/psum | solution.py:37
  115.2 6.6 %psum.30 = s32[16]{0:T(128)S(1)} all-reduce(s32[16]{0:T(128)S(1)} %psum.29), channel_id=1, replica_groups=mesh['fsdp_0'=8,'fsdp_1'=8,'fsdp_2'=2,'dp'=4] {'fsdp_2'}, use_global_device_ids=true, to_apply=%region_2.0 | all-reduce | flops 16 | bytes 128 | tf_op jit(solution)/shard_map/psum | solution.py:37
  121.8 7.3 %psum.31 = s32[16]{0:T(128)S(1)} all-reduce(s32[16]{0:T(128)S(1)} %psum.30), channel_id=1, replica_groups=mesh['fsdp_0'=8,'fsdp_1'=8,'fsdp_2'=2,'dp'=4] {'dp'}, use_global_device_ids=true, to_apply=%region_3.0 | all-reduce | flops 16 | bytes 128 | tf_op jit(solution)/shard_map/psum | solution.py:37
  129.1 0.1 broadcast_in_dim.34
  129.2 0.1 broadcast_in_dim.35
  129.3 0.2 reduce_sum.9
  129.5 3.1 %fusion.4 = (bf16[32,5120]{1,0:T(8,128)(2,1)S(1)}, f32[32,5120]{1,0:T(8,128)}, f32[32,5120]{1,0:T(8,128)}, f32[32,5120]{1,0:T(8,128)}) fusion(f32[32,5120]{1,0:T(8,128)} %param.10, f32[5120]{0:T(1024)S(1)} %sub.30, f32[32,5120]{1,0:T(8,128)S(1)} %reduce_sum.9, f32[32,5120]{1,0:T(8,128)} %param.12, f32[5120]{0:T(1024)S(1)} %sub.28, f32[32,5120]{1,0:T(8,128)} %param.11, ...), kind=kLoop, calls=%fused_computation.12 | loop fusion | flops 2785280 | bytes 4961284 | tf_op jit(solution)/shard_map/convert_element_type | solution.py:74
  132.6 1.9 all_to_all.18
  134.5 0.7 copy.32
  135.2 2.4 %reshape.56 = bf16[128,2,640]{2,1,0:T(2,128)(2,1)} reshape(bf16[128,32,40]{2,1,0:T(8,128)(2,1)S(1)} %bitcast.30) | data formatting | bytes 655360
  137.6 10.5 %all-to-all-start.1 = ((bf16[128,2,640]{2,1,0:T(2,128)(2,1)}), bf16[128,2,640]{2,1,0:T(2,128)(2,1)S(1)}, u32[]{:S(2)}, u32[]{:S(2)}) async-start(bf16[128,2,640]{2,1,0:T(2,128)(2,1)} %reshape.56), calls=%async_computation.1 | async-start | bytes 655360 | tf_op jit(solution)/shard_map/all_to_all | solution.py:76
  148.0 0.5 convert_add_fusion
  148.6 15.3 %all-to-all-done.1 = bf16[128,2,640]{2,1,0:T(2,128)(2,1)S(1)} async-done(((bf16[128,2,640]{2,1,0:T(2,128)(2,1)}), bf16[128,2,640]{2,1,0:T(2,128)(2,1)S(1)}, u32[]{:S(2)}, u32[]{:S(2)}) %all-to-all-start.1) | async-done | bytes 327712 | tf_op jit(solution)/shard_map/all_to_all | solution.py:76
  163.9 1.6 reshape.57
  165.5 13.2 %all-gather.6.cloned.1.call-done = bf16[128,4096]{0,1:T(8,128)(2,1)} async-done(((bf16[128,32]{0,1:T(8,128)(2,1)}), bf16[128,4096]{0,1:T(8,128)(2,1)}) %all-gather.6.cloned.1.call-update) | async-done | bytes 1048592 | tf_op jit(solution)/shard_map/all_gather | solution.py:78
  178.7 2.3 %fusion = bf16[128,40]{0,1:T(8,128)(2,1)} fusion(bf16[4096,40]{1,0:T(8,128)(2,1)S(1)} %bitcast.29, bf16[128,4096]{0,1:T(8,128)(2,1)} %all-gather.6.cloned.1.call-done), kind=kOutput, calls=%fused_computation.1 | convolution fusion | flops 41948160 | bytes 1386496 | tf_op jit(solution)/shard_map/dot_general | solution.py:77
  (11 shorter events, 0.0 us)
Async XLA Ops:
  8.0 74.6 %all-gather.4.cloned.1.call-start = ((), (), s32[]{:S(2)}) async-start(), calls=%async_computation.2 | async-start | bytes 1966080 | tf_op jit(solution)/shard_map/all_gather | solution.py:24
  82.6 2.2 %copy-start.1 = (bf16[128,32]{0,1:T(8,128)(2,1)S(1)}, bf16[128,32]{0,1:T(8,128)(2,1)}, u32[]{:S(2)}) copy-start(bf16[128,32]{0,1:T(8,128)(2,1)} %param.8) | copy-start | bytes 24580
  87.1 4.4 %copy-start.3 = (s32[16]{0:T(128)S(1)}, s32[16]{0:T(128)}, u32[]{:S(2)}) copy-start(s32[16]{0:T(128)} %param.14) | copy-start | bytes 196
  87.1 5.4 %copy-start.2 = (s32[1,16]{1,0:T(1,128)S(1)}, s32[1,16]{1,0:T(1,128)}, u32[]{:S(2)}) copy-start(s32[1,16]{1,0:T(1,128)} %param.13) | copy-start | bytes 196
  87.1 42.2 %all-to-all-start = ((f32[4,32,5120]{2,1,0:T(8,128)}), f32[4,32,5120]{2,1,0:T(8,128)S(1)}, u32[]{:S(2)}, u32[]{:S(2)}) async-start(f32[4,32,5120]{2,1,0:T(8,128)} %broadcast_in_dim.38), calls=%async_computation | async-start | bytes 5242880 | tf_op jit(solution)/shard_map/all_to_all | solution.py:43
  90.9 87.8 %all-gather.6.cloned.1.call-start = ((), (), s32[]{:S(2)}) async-start(), calls=%async_computation.3 | async-start | bytes 1056768 | tf_op jit(solution)/shard_map/all_gather | solution.py:78
  132.6 2.6 %copy-start = (bf16[32,5120]{1,0:T(8,128)(2,1)}, bf16[32,5120]{1,0:T(8,128)(2,1)S(1)}, u32[]{:S(2)}) copy-start(bf16[32,5120]{1,0:T(8,128)(2,1)S(1)} %get-tuple-element.6) | copy-start | bytes 983044
  137.6 26.3 %all-to-all-start.1 = ((bf16[128,2,640]{2,1,0:T(2,128)(2,1)}), bf16[128,2,640]{2,1,0:T(2,128)(2,1)S(1)}, u32[]{:S(2)}, u32[]{:S(2)}) async-start(bf16[128,2,640]{2,1,0:T(2,128)(2,1)} %reshape.56), calls=%async_computation.1 | async-start | bytes 655360 | tf_op jit(solution)/shard_map/all_to_all | solution.py:76
Sparse Core Ops, SparseCore 0:
  56.2 26.3 all-gather.3
Sparse Core Ops, SparseCore 1:
  94.4 84.3 all-gather.5
where the time goes:
time: 189 us; the launch traced here: 188 us
  blocking collectives  83.7 us (44%)
  waiting for transfers between devices  55.6 us (29%)
  between operations  16.2 us (9%)
  starting transfers between devices  14.3 us (8%)
  local copies, waits for them, and re-layouts  12 us (6%)
  other arithmetic  3.83 us (2%)
  matrix products  2.8 us (1%)
    all_gather x1, blocking collectives, all_blocks(): blocks = lax.all_gather(blocks, axes[k], axis=0, tiled=True)  47 us
    psum x4, blocking collectives, over_axes(): x = lax.psum(x, axis)  36.6 us
    all_gather x1, waiting for transfers between devices, all_blocks(): blocks = lax.all_gather(blocks, axes[k], axis=0, tiled=True)  26.5 us
    all_to_all x1, waiting for transfers between devices, local(): lax.all_to_all(weight_half, FSDP, split_axis=1, concat_axis=0, tiled=True)  15.3 us
    all_gather x1, waiting for transfers between devices, local(): lax.all_gather(tokens, FSDP, axis=1, tiled=True)  13.2 us
    all_to_all x1, starting transfers between devices, local(): lax.all_to_all(weight_half, FSDP, split_axis=1, concat_axis=0, tiled=True)  10.5 us
    unnamed x11, local copies, waits for them, and re-layouts  4.98 us
    all_to_all x1, starting transfers between devices, from_everyone(): lax.all_to_all(jnp.broadcast_to(x[None], (size, *x.shape)), axis, 0, 0, t...  3.78 us
  transfers between devices with their start and end apart: 4, of which 3 were waited for; matrix products, arithmetic and copies ran while one was open for 5% of the time, Pallas kernels for 0%

commit v1 on v0

--- a/solution.py
+++ b/solution.py
@@ -21,7 +21,9 @@
 def all_blocks(x, axes, order):
     blocks = x[None]
     for k in order:
-        blocks = lax.all_gather(blocks, axes[k], axis=0, tiled=True)
+        blocks = jnp.concatenate(
+            lax.all_to_all(jnp.stack([blocks] * lax.axis_size(axes[k])), axes[k], 0, 0), axis=0
+        )
     current = [lax.axis_size(axes[k]) for k in reversed(order)]
     blocks = blocks.reshape(*current, *x.shape)
     turned = sorted(range(len(order)), key=lambda place: order[len(order) - 1 - place])

time: 189 us -> 150 us (0.79)
  waiting for transfers between devices: 55.6 us -> 25 us
  blocking collectives: 83.7 us -> 76.9 us
    all_gather x1 -> x0, blocking collectives: 47 us -> none  [all_blocks(): blocks = lax.all_gather(blocks, axes[k], axis=0, tiled=True)]
    all_to_all x0 -> x2, blocking collectives: none -> 43.5 us  [all_blocks(): lax.all_to_all(jnp.stack([blocks] * lax.axis_size(axes[k])), axes[k], 0, 0)]
    all_gather x1 -> x0, waiting for transfers between devices: 26.5 us -> none  [all_blocks(): blocks = lax.all_gather(blocks, axes[k], axis=0, tiled=True)]
    all_gather x1, waiting for transfers between devices: 13.2 us -> 8.97 us  [local(): lax.all_gather(tokens, FSDP, axis=1, tiled=True)]
    psum x4, blocking collectives: 36.6 us -> 33.4 us  [over_axes(): x = lax.psum(x, axis)]
    transpose x1 -> x0, local copies, waits for them, and re-layouts: 2.18 us -> none  [all_blocks(): blocks.transpose(*turned, *range(len(order), blocks.ndim))]
    unnamed x11 -> x10, local copies, waits for them, and re-layouts: 4.98 us -> 4.55 us
  transfers between devices with their start and end apart: 4 -> 3, of which waited for: 3 -> 2; matrix products, arithmetic and copies ran while one was open for 5% -> 6% of each run, Pallas kernels for 0% -> 0%
where the time goes in v1:
time: 150 us; the launch traced here: 149 us
  blocking collectives  76.9 us (51%)
  waiting for transfers between devices  25 us (17%)
  starting transfers between devices  15.5 us (10%)
  between operations  14.8 us (10%)
  local copies, waits for them, and re-layouts  10.3 us (7%)
  other arithmetic  3.94 us (3%)
  matrix products  2.79 us (2%)
    all_to_all x2, blocking collectives, all_blocks(): lax.all_to_all(jnp.stack([blocks] * lax.axis_size(axes[k])), axes[k], 0, 0)  43.5 us
    psum x4, blocking collectives, over_axes(): x = lax.psum(x, axis)  33.4 us
    all_to_all x1, waiting for transfers between devices, local(): lax.all_to_all(weight_half, FSDP, split_axis=1, concat_axis=0, tiled=True)  15.4 us
    all_to_all x1, starting transfers between devices, local(): lax.all_to_all(weight_half, FSDP, split_axis=1, concat_axis=0, tiled=True)  11.3 us
    all_gather x1, waiting for transfers between devices, local(): lax.all_gather(tokens, FSDP, axis=1, tiled=True)  8.97 us
    unnamed x10, local copies, waits for them, and re-layouts  4.55 us
    all_to_all x1, starting transfers between devices, from_everyone(): lax.all_to_all(jnp.broadcast_to(x[None], (size, *x.shape)), axis, 0, 0, t...  4.15 us
    convert_element_type x1, other arithmetic, local(): weight_half = master_next.astype(jnp.bfloat16)  3.1 us
  transfers between devices with their start and end apart: 3, of which 2 were waited for; matrix products, arithmetic and copies ran while one was open for 6% of the time, Pallas kernels for 0%

profile of v1, /device:TPU:1, one launch (start us, length us, event | category | flops | bytes accessed | tf_op | source)
XLA Modules:
  0.0 149.2 jit_solution(17327392842892053294)
XLA Ops:
  7.2 0.8 stack.6
  8.0 35.5 %all_to_all.34 = bf16[64,1,128,40]{2,3,1,0:T(8,128)(2,1)S(1)} all-to-all(bf16[64,1,128,40]{2,3,1,0:T(8,128)(2,1)S(1)} %stack.6), channel_id=1, replica_groups=mesh['fsdp_0'=8,'fsdp_1'=8,'fsdp_2'=2,'dp'=4] {'fsdp_0','fsdp_1'}, dimensions={0} | all-to-all | bytes 1310720 | tf_op jit(solution)/shard_map/all_to_all | solution.py:25
  43.5 0.1 pad_maximum_fusion
  43.6 8.0 %all_to_all.35 = bf16[2,64,128,40]{2,3,1,0:T(8,128)(2,1)S(1)} all-to-all(bf16[2,64,128,40]{2,3,1,0:T(8,128)(2,1)S(1)} %pad_maximum_fusion), channel_id=1, replica_groups=mesh['fsdp_0'=8,'fsdp_1'=8,'fsdp_2'=2,'dp'=4] {'fsdp_2'}, dimensions={0} | all-to-all | bytes 2621440 | tf_op jit(solution)/shard_map/all_to_all | solution.py:25
  51.6 0.1 copy.19
  51.7 0.6 copy-done.1
  52.3 0.5 convolution_bitcast_fusion
  52.8 1.8 %broadcast_in_dim.34 = f32[4,32,5120]{2,1,0:T(8,128)} broadcast(f32[32,5120]{1,0:T(8,128)S(1)} %convolution_bitcast_fusion), dimensions={1,2} | broadcast | bytes 3276800 | tf_op jit(solution)/shard_map/broadcast_in_dim | solution.py:45
  54.6 4.1 %all-to-all-start.2 = ((f32[4,32,5120]{2,1,0:T(8,128)}), f32[4,32,5120]{2,1,0:T(8,128)S(1)}, u32[]{:S(2)}, u32[]{:S(2)}) async-start(f32[4,32,5120]{2,1,0:T(8,128)} %broadcast_in_dim.34), calls=%async_computation.2 | async-start | bytes 5242880 | tf_op jit(solution)/shard_map/all_to_all | solution.py:45
  58.7 0.7 all-gather.2.cloned.1.call-update
  59.5 0.1 broadcast_in_dim.36
  59.6 0.1 sub.30
  59.6 0.1 broadcast_in_dim.35
  59.7 0.1 sub.28
  60.5 10.4 %psum.28 = s32[16]{0:T(128)S(1)} all-reduce(s32[16]{0:T(128)S(1)} %bitcast.30), channel_id=1, replica_groups=mesh['fsdp_0'=8,'fsdp_1'=8,'fsdp_2'=2,'dp'=4] {'fsdp_0'}, use_global_device_ids=true, to_apply=%region_0.0 | all-reduce | flops 16 | bytes 128 | tf_op jit(solution)/shard_map/psum | solution.py:39
  70.8 8.9 %psum.29 = s32[16]{0:T(128)S(1)} all-reduce(s32[16]{0:T(128)S(1)} %psum.28), channel_id=1, replica_groups=mesh['fsdp_0'=8,'fsdp_1'=8,'fsdp_2'=2,'dp'=4] {'fsdp_1'}, use_global_device_ids=true, to_apply=%region_1.0 | all-reduce | flops 16 | bytes 128 | tf_op jit(solution)/shard_map/psum | solution.py:39
  79.7 6.7 %psum.30 = s32[16]{0:T(128)S(1)} all-reduce(s32[16]{0:T(128)S(1)} %psum.29), channel_id=1, replica_groups=mesh['fsdp_0'=8,'fsdp_1'=8,'fsdp_2'=2,'dp'=4] {'fsdp_2'}, use_global_device_ids=true, to_apply=%region_2.0 | all-reduce | flops 16 | bytes 128 | tf_op jit(solution)/shard_map/psum | solution.py:39
  86.4 7.5 %psum.31 = s32[16]{0:T(128)S(1)} all-reduce(s32[16]{0:T(128)S(1)} %psum.30), channel_id=1, replica_groups=mesh['fsdp_0'=8,'fsdp_1'=8,'fsdp_2'=2,'dp'=4] {'dp'}, use_global_device_ids=true, to_apply=%region_3.0 | all-reduce | flops 16 | bytes 128 | tf_op jit(solution)/shard_map/psum | solution.py:39
  93.9 0.1 broadcast_in_dim.31
  94.0 0.1 broadcast_in_dim.32
  94.1 0.0 all-to-all-done.2
  94.1 0.2 reduce_sum.9
  94.3 3.1 %fusion.4 = (bf16[32,5120]{1,0:T(8,128)(2,1)S(1)}, f32[32,5120]{1,0:T(8,128)}, f32[32,5120]{1,0:T(8,128)}, f32[32,5120]{1,0:T(8,128)}) fusion(f32[32,5120]{1,0:T(8,128)} %param.10, f32[5120]{0:T(1024)S(1)} %sub.30, f32[32,5120]{1,0:T(8,128)S(1)} %reduce_sum.9, f32[32,5120]{1,0:T(8,128)} %param.12, f32[5120]{0:T(1024)S(1)} %sub.28, f32[32,5120]{1,0:T(8,128)} %param.11, ...), kind=kLoop, calls=%fused_computation.14 | loop fusion | flops 2785280 | bytes 4961284 | tf_op jit(solution)/shard_map/convert_element_type | solution.py:76
  97.4 1.9 %all_to_all.26 = bf16[32,128,40]{2,1,0:T(8,128)(2,1)S(1)} reshape(bf16[32,5120]{1,0:T(8,128)(2,1)S(1)} %get-tuple-element.6) | data formatting | bytes 655360 | tf_op jit(solution)/shard_map/all_to_all | solution.py:78
  99.3 0.7 copy.24
  100.0 2.3 %reshape.53 = bf16[128,2,640]{2,1,0:T(2,128)(2,1)} reshape(bf16[128,32,40]{2,1,0:T(8,128)(2,1)S(1)} %bitcast.28) | data formatting | bytes 655360
  102.3 11.3 %all-to-all-start.3 = ((bf16[128,2,640]{2,1,0:T(2,128)(2,1)}), bf16[128,2,640]{2,1,0:T(2,128)(2,1)S(1)}, u32[]{:S(2)}, u32[]{:S(2)}) async-start(bf16[128,2,640]{2,1,0:T(2,128)(2,1)} %reshape.53), calls=%async_computation.3 | async-start | bytes 655360 | tf_op jit(solution)/shard_map/all_to_all | solution.py:78
  113.7 0.5 convert_add_fusion
  114.2 15.4 %all-to-all-done.3 = bf16[128,2,640]{2,1,0:T(2,128)(2,1)S(1)} async-done(((bf16[128,2,640]{2,1,0:T(2,128)(2,1)}), bf16[128,2,640]{2,1,0:T(2,128)(2,1)S(1)}, u32[]{:S(2)}, u32[]{:S(2)}) %all-to-all-start.3) | async-done | bytes 327712 | tf_op jit(solution)/shard_map/all_to_all | solution.py:78
  129.5 1.6 %reshape.54 = bf16[128,32,40]{2,1,0:T(8,128)(2,1)S(1)} reshape(bf16[128,2,640]{2,1,0:T(2,128)(2,1)S(1)} %all-to-all-done.3) | data formatting | bytes 655360
  131.2 9.0 %all-gather.2.cloned.1.call-done = bf16[128,4096]{0,1:T(8,128)(2,1)} async-done(((bf16[128,32]{0,1:T(8,128)(2,1)}), bf16[128,4096]{0,1:T(8,128)(2,1)}) %all-gather.2.cloned.1.call-update) | async-done | bytes 1048592 | tf_op jit(solution)/shard_map/all_gather | solution.py:80
  140.1 2.3 %fusion = bf16[128,40]{0,1:T(8,128)(2,1)} fusion(bf16[4096,40]{1,0:T(8,128)(2,1)S(1)} %bitcast.27, bf16[128,4096]{0,1:T(8,128)(2,1)} %all-gather.2.cloned.1.call-done), kind=kOutput, calls=%fused_computation.3 | convolution fusion | flops 41948160 | bytes 1386496 | tf_op jit(solution)/shard_map/dot_general | solution.py:79
  (10 shorter events, 0.0 us)
Async XLA Ops:
  51.6 0.7 copy-start.1
  54.6 4.9 %copy-start.3 = (s32[16]{0:T(128)S(1)}, s32[16]{0:T(128)}, u32[]{:S(2)}) copy-start(s32[16]{0:T(128)} %param.14) | copy-start | bytes 196
  54.6 5.9 %copy-start.2 = (s32[1,16]{1,0:T(1,128)S(1)}, s32[1,16]{1,0:T(1,128)}, u32[]{:S(2)}) copy-start(s32[1,16]{1,0:T(1,128)} %param.13) | copy-start | bytes 196
  54.6 39.5 %all-to-all-start.2 = ((f32[4,32,5120]{2,1,0:T(8,128)}), f32[4,32,5120]{2,1,0:T(8,128)S(1)}, u32[]{:S(2)}, u32[]{:S(2)}) async-start(f32[4,32,5120]{2,1,0:T(8,128)} %broadcast_in_dim.34), calls=%async_computation.2 | async-start | bytes 5242880 | tf_op jit(solution)/shard_map/all_to_all | solution.py:45
  58.7 81.4 %all-gather.2.cloned.1.call-start = ((), (), s32[]{:S(2)}) async-start(), calls=%async_computation.4 | async-start | bytes 1056768 | tf_op jit(solution)/shard_map/all_gather | solution.py:80
  97.4 2.6 %copy-start = (bf16[32,5120]{1,0:T(8,128)(2,1)}, bf16[32,5120]{1,0:T(8,128)(2,1)S(1)}, u32[]{:S(2)}) copy-start(bf16[32,5120]{1,0:T(8,128)(2,1)S(1)} %get-tuple-element.6) | copy-start | bytes 983044
  102.3 27.2 %all-to-all-start.3 = ((bf16[128,2,640]{2,1,0:T(2,128)(2,1)}), bf16[128,2,640]{2,1,0:T(2,128)(2,1)S(1)}, u32[]{:S(2)}, u32[]{:S(2)}) async-start(bf16[128,2,640]{2,1,0:T(2,128)(2,1)} %reshape.53), calls=%async_computation.3 | async-start | bytes 655360 | tf_op jit(solution)/shard_map/all_to_all | solution.py:78
Sparse Core Ops, SparseCore 0:
  62.6 77.5 all-gather.1
